TPU v7x, 256 devices: a whole 4x4x8 slice. The times are simulated.
256 devices in a mesh: batch: 32 (over x, z_hi, core), hidden: 8 (over z_lo, y).
Axes of the slice: x: 4, y: 4, z: 8 (z_hi: 4, z_lo: 2; z = z_hi * 2 + z_lo), core: 2. Of those that a mesh axis runs over, the one named last changes fastest.
Arguments:
- features: bfloat16 [12288, 512], P('batch'), may hold values from -6 to 6
- w_first: bfloat16 [512, 8192], P('batch', 'hidden'), may hold values from -0.25 to 0.25
- w_second: bfloat16 [8192, 4096], P('hidden', 'batch'), may hold values from -0.0625 to 0.0625
- w_head: bfloat16 [4096, 8], P('hidden'), may hold values from -0.09375 to 0.09375
- rewards: float32 [8, 12288], P(None, 'batch'), may hold values from -1.75 to 1.75
- discount: float32 [8], replicated, as said below
- trace: float32 [8], replicated, as said below
- episode: int32 [12288], P('batch'), may hold values from 0 to 32, as said below
Outputs:
- advantages: float32 [8, 12288], P(None, 'batch')
- loss: float32 [], replicated
- grad_first: float32 [512, 8192], P('batch', 'hidden')
- grad_second: float32 [8192, 4096], P('hidden', 'batch')
- grad_head: float32 [4096, 8], P('hidden')
Inputs may be any that keep to these rules, and one draw needn't show every extreme that they name: Each discount lies between 0.875 and 1. Each trace factor lies between 0.875 and 1. episode numbers never fall along the rollout and rise by one at each episode start; each block of 384 timesteps of one index of batch holds exactly one episode start besides the rollout's own start at timestep 0, and that start never falls on the block's first timestep; the rollout begins with episode 0.
All inputs are finite; a program needn't handle non-finite values.
Results may differ from a plain program's by a relative error of at most 0.018.
Values may be sent and summed in bfloat16 or wider, within the bound.
A program may use at most 128 MiB of HBM per device.

v0:
```python
import jax
import jax.numpy as jnp
from jax import lax
from jax.sharding import PartitionSpec as P


def sent_to_all(array, axis):
    length = lax.axis_size(axis)
    return lax.all_to_all(
        jnp.broadcast_to(array[None], (length, *array.shape)), axis, 0, 0, tiled=True
    )


def over_copies(array, axis):
    return sent_to_all(array, axis).sum(axis=0)


def passed_along(value, axis, steps):
    count = lax.axis_size(axis)
    initial, last = (max(0, -steps), min(count, count - steps))
    return lax.ppermute(value, axis, [(source, source + steps) for source in range(initial, last)])


def collected_together(array, axis):
    leaves = jax.tree.leaves(array)
    turns = sorted(range(len(leaves)), key=lambda k: -leaves[k].size)
    width = (1, *leaves[turns[0]].shape)[-1]
    lines = [
        jnp.pad(leaves[k].reshape(-1), (0, -leaves[k].size % width)).reshape(-1, width)
        for k in turns
    ]
    both, at, found = (sent_to_all(jnp.concatenate(lines), axis), 0, {})
    for k, line in zip(turns, lines):
        share = both[:, at : at + len(line)].reshape(len(both), -1)
        found[k] = share[:, : leaves[k].size].reshape(-1, *leaves[k].shape)
        at += len(line)
    numbers = iter(range(len(leaves)))
    return jax.tree.map(lambda _: found[next(numbers)], array)


def joined_by_halves(pieces, combine):
    while len(jax.tree.leaves(pieces)[0]) > 1:
        pieces = jax.vmap(combine)(
            *(jax.tree.map(lambda part: part[side::2], pieces) for side in (0, 1))
        )
    return jax.tree.map(lambda part: part[0], pieces)


def prefix(array, axis, combine, identity):
    length, position = (lax.axis_size(axis), lax.axis_index(axis))
    passed = jnp.arange(length) > position

    def kept(part, zero, own):
        part = jnp.where(
            passed.reshape(-1, *(1 for _ in own.shape)), part, jnp.asarray(zero, own.dtype)
        )
        return part[::-1]

    pieces = collected_together(array, axis)
    return joined_by_halves(jax.tree.map(kept, pieces, identity, array), combine)


def cut_along(array, dim, length):
    before, after = (array.shape[:dim], array.shape[dim + 1 :])
    return jnp.moveaxis(array.reshape(*before, length, -1, *after), dim, 0)


def summed_on_arrival(array, axis, dim):
    length = lax.axis_size(axis)
    pieces = lax.all_to_all(cut_along(array, dim, length), axis, 0, 0, tiled=True)
    return jnp.sum(pieces.astype(jnp.float32), axis=0)


def chain_maps(farther, nearer):
    return (farther[0] * nearer[0], nearer[1] + nearer[0] * farther[1])


def silu_slope(value):
    sigmoid_value = jax.nn.sigmoid(value)
    return sigmoid_value * (1.0 + value * (1.0 - sigmoid_value))


def contract(left, right, left_dim, right_dim):
    return lax.dot_general(
        left, right, (((left_dim,), (right_dim,)), ((), ())), preferred_element_type=jnp.float32
    )


def shards(features, w_first, w_second, w_head, rewards, discount, trace, episode):
    rows_here = features.shape[0]
    heads = w_head.shape[1]
    columns = features
    pre_first = jnp.dot(
        columns,
        lax.all_gather(w_first, "batch", axis=0, tiled=True),
        preferred_element_type=jnp.float32,
    )
    hidden_first = jax.nn.silu(pre_first).astype(jnp.bfloat16)
    partial_value = jnp.dot(
        hidden_first,
        lax.all_gather(w_second, "batch", axis=1, tiled=True),
        preferred_element_type=jnp.float32,
    )
    pre_second = lax.psum_scatter(
        partial_value.astype(jnp.bfloat16), "hidden", scatter_dimension=1, tiled=True
    ).astype(jnp.float32)
    hidden_second = jax.nn.silu(pre_second).astype(jnp.bfloat16)
    values = over_copies(
        jnp.dot(hidden_second, w_head, preferred_element_type=jnp.float32), "hidden"
    )
    values_t = values.T
    next_value = passed_along(values_t[:, :1], "batch", -1)
    next_first = passed_along(episode[:1] + 1, "batch", -1)
    following = jnp.concatenate([episode[1:] + 1, next_first])
    keep = (following == episode + 1).astype(jnp.float32)
    value_after = jnp.concatenate([values_t[:, 1:], next_value], axis=1)
    delta = rewards + discount[:, None] * keep[None, :] * value_after - values_t
    factor = discount[:, None] * trace[:, None] * keep[None, :]
    reach, local_adv = lax.associative_scan(chain_maps, (factor, delta), reverse=True, axis=1)
    identity = (jnp.ones((heads,), jnp.float32), jnp.zeros((heads,), jnp.float32))
    _, entering = prefix((reach[:, 0], local_adv[:, 0]), "batch", chain_maps, identity)
    advantages = local_adv + reach * entering[:, None]
    slope_value = (-advantages.T).astype(jnp.bfloat16)
    slope_share = (contract(slope_value, w_head, 1, 1) * silu_slope(pre_second)).astype(
        jnp.bfloat16
    )
    slope_second = lax.all_gather(slope_share, "hidden", axis=1, tiled=True)
    head_term = contract(hidden_second, slope_value, 0, 0)
    grad_head, loss_sum = (
        over_copies(head_term, "batch"),
        over_copies(jnp.sum(advantages * advantages), "batch"),
    )
    loss = 0.5 * loss_sum / (rows_here * lax.axis_size("batch") * heads)
    columns = slope_second
    back_first = contract(columns, lax.all_gather(w_second, "batch", axis=1, tiled=True), 1, 1)
    slope_first = (back_first * silu_slope(pre_first)).astype(jnp.bfloat16)
    columns = slope_second
    grad_second = (
        lax.psum_scatter(
            contract(columns, hidden_first, 0, 0).astype(jnp.bfloat16),
            "batch",
            scatter_dimension=0,
            tiled=True,
        )
        .astype(jnp.float32)
        .T
    )
    columns = features
    grad_first = summed_on_arrival(
        contract(columns, slope_first, 0, 0).astype(jnp.bfloat16), "batch", 0
    )
    return (advantages, loss, grad_first, grad_second, grad_head)


def solution(mesh):
    placed = (
        P("batch", None),
        P("batch", "hidden"),
        P("hidden", "batch"),
        P("hidden", None),
        P(None, "batch"),
        P(),
        P(),
        P("batch"),
    )
    return jax.shard_map(
        shards,
        mesh=mesh,
        in_specs=placed,
        out_specs=(
            P(None, "batch"),
            P(),
            P("batch", "hidden"),
            P("hidden", "batch"),
            P("hidden", None),
        ),
        check_vma=False,
    )
```

profile of v0, /device:TPU:8, one launch (start us, length us, event | category | flops | bytes accessed | tf_op | source)
XLA Modules:
  0.0 450.4 jit_solution(7222530237722029714)
XLA Ops:
  7.2 0.7 all-gather.4.cloned.1.call-update
  8.0 0.7 all-gather.6.cloned.1.call-update
  8.7 56.7 %all-gather.4.cloned.1.call-done = bf16[512,1024]{1,0:T(8,128)(2,1)} async-done(((bf16[16,1024]{1,0:T(8,128)(2,1)}), bf16[512,1024]{1,0:T(8,128)(2,1)}) %all-gather.4.cloned.1.call-update) | async-done | bytes 1048592 | tf_op jit(solution)/shard_map/all_gather | solution.py:95
  65.5 1.8 fusion.20
  67.3 82.4 %all-gather.6.cloned.1.call-done = bf16[1024,4096]{1,0:T(8,128)(2,1)} async-done(((bf16[1024,128]{1,0:T(8,128)(2,1)}), bf16[1024,4096]{1,0:T(8,128)(2,1)}) %all-gather.6.cloned.1.call-update) | async-done | bytes 8388624 | tf_op jit(solution)/shard_map/all_gather | solution.py:101
  149.7 8.2 %convolution_convert_fusion.1 = bf16[384,4096]{1,0:T(8,128)(2,1)} fusion(bf16[1024,4096]{1,0:T(8,128)(2,1)} %all-gather.6.cloned.1.call-done, f32[384,1024]{1,0:T(8,128)S(1)} %fusion.20), kind=kOutput, calls=%fused_computation.1 | convolution fusion | flops 3224764416 | bytes 13107200 | tf_op jit(solution)/shard_map/dot_general | solution.py:99
  157.9 0.6 copy-done.5
  158.6 0.5 slice.355
  159.7 1.3 collective-permute-start
  161.1 43.1 %reduce-scatter.3.cloned.1.call-done = bf16[384,512]{1,0:T(8,128)(2,1)} async-done(((bf16[384,4096]{1,0:T(8,128)(2,1)}), bf16[384,512]{1,0:T(8,128)(2,1)}) %reduce-scatter.3.cloned.1.call-update) | async-done | bytes 393232 | tf_op jit(solution)/shard_map/reduce_scatter | solution.py:104
  204.3 1.2 fusion.4
  205.7 0.7 broadcast_in_dim.26
  206.4 5.4 %all-to-all-start = ((f32[8,384,8]{1,2,0:T(8,128)}), f32[8,384,8]{1,2,0:T(8,128)S(1)}, u32[]{:S(2)}, u32[]{:S(2)}) async-start(f32[8,384,8]{1,2,0:T(8,128)} %broadcast_in_dim.26), calls=%async_computation.1 | async-start | bytes 196608 | tf_op jit(solution)/shard_map/all_to_all | solution.py:9
  211.8 0.6 fusion.12
  212.4 4.4 all-to-all-done
  216.9 1.3 collective-permute-start.1
  218.2 1.8 collective-permute-done.1
  220.1 0.3 slice.371
  220.4 0.3 slice.365
  220.6 0.3 slice.361
  221.9 0.3 slice.367
  222.2 0.3 slice.363
  222.4 0.3 slice.359
  230.9 0.3 pad.113
  231.3 0.3 pad.128
  231.7 0.3 pad.112
  232.6 0.6 broadcast_in_dim.28
  233.3 9.6 %all-to-all-start.1 = ((f32[32,2,8]{2,1,0:T(2,128)}), f32[32,2,8]{2,1,0:T(2,128)S(1)}, u32[]{:S(2)}, u32[]{:S(2)}) async-start(f32[32,2,8]{2,1,0:T(2,128)} %broadcast_in_dim.28), calls=%async_computation.2 | async-start | bytes 65536 | tf_op jit(solution)/shard_map/all_to_all | solution.py:9
  243.4 9.3 %all-to-all-done.1 = f32[32,2,8]{2,1,0:T(2,128)S(1)} async-done(((f32[32,2,8]{2,1,0:T(2,128)}), f32[32,2,8]{2,1,0:T(2,128)S(1)}, u32[]{:S(2)}, u32[]{:S(2)}) %all-to-all-start.1) | async-done | bytes 2080 | tf_op jit(solution)/shard_map/all_to_all | solution.py:9
  253.2 0.7 multiply_reduce_fusion
  253.9 1.2 fusion
  255.1 39.2 %all-gather.8.cloned.1.call-done = bf16[384,4096]{1,0:T(8,128)(2,1)} async-done(((bf16[384,512]{1,0:T(8,128)(2,1)}), bf16[384,4096]{1,0:T(8,128)(2,1)}) %all-gather.8.cloned.1.call-update) | async-done | bytes 3145744 | tf_op jit(solution)/shard_map/all_gather | solution.py:127
  294.4 8.8 %convolution_convert_fusion = bf16[4096,1024]{1,0:T(8,128)(2,1)} fusion(bf16[384,4096]{1,0:T(8,128)(2,1)} %all-gather.8.cloned.1.call-done, f32[384,1024]{1,0:T(8,128)S(1)} %fusion.20), kind=kOutput, calls=%fused_computation | convolution fusion | flops 3227385856 | bytes 13107200 | tf_op jit(solution)/shard_map/dot_general | solution.py:84
  303.2 1.3 broadcast_in_dim.52
  304.5 9.1 %all-to-all-start.2 = ((f32[32,1,1]{2,1,0:T(1,128)}), f32[32,1,1]{2,1,0:T(1,128)S(1)}, u32[]{:S(2)}, u32[]{:S(2)}) async-start(f32[32,1,1]{2,1,0:T(1,128)} %broadcast_in_dim.52), calls=%async_computation.3 | async-start | bytes 32768 | tf_op jit(solution)/shard_map/all_to_all | solution.py:9
  313.8 9.6 %all-to-all-done.2 = f32[32,1,1]{2,1,0:T(1,128)S(1)} async-done(((f32[32,1,1]{2,1,0:T(1,128)}), f32[32,1,1]{2,1,0:T(1,128)S(1)}, u32[]{:S(2)}, u32[]{:S(2)}) %all-to-all-start.2) | async-done | bytes 160 | tf_op jit(solution)/shard_map/all_to_all | solution.py:9
  323.3 0.9 broadcast_in_dim.53
  324.2 3.9 all-to-all-start.4
  328.1 10.0 %convolution_convert_fusion.2 = bf16[1024,512]{0,1:T(8,128)(2,1)} fusion(bf16[384,512]{1,0:T(8,128)(2,1)S(1)} %copy-done, f32[384,1024]{1,0:T(8,128)S(1)} %fusion.20, bf16[384,4096]{1,0:T(8,128)(2,1)} %all-gather.8.cloned.1.call-done, bf16[1024,4096]{1,0:T(8,128)(2,1)} %all-gather.6.cloned.1.call-done), kind=kOutput, calls=%fused_computation.6 | convolution fusion | flops 3627941888 | bytes 14548992 | tf_op jit(solution)/shard_map/dot_general | solution.py:84
  338.1 8.0 %all-to-all-done.4 = f32[32,512,8]{1,2,0:T(8,128)S(1)} async-done(((f32[32,512,8]{1,2,0:T(8,128)}), f32[32,512,8]{1,2,0:T(8,128)S(1)}, u32[]{:S(2)}, u32[]{:S(2)}) %all-to-all-start.4) | async-done | bytes 524320 | tf_op jit(solution)/shard_map/all_to_all | solution.py:9
  346.1 4.3 all-to-all-start.3
  350.5 0.6 reduce_sum.47
  351.8 0.7 reduce_sum.49
  352.4 28.6 %all-to-all-done.3 = bf16[32,16,1024]{2,1,0:T(8,128)(2,1)S(1)} async-done(((bf16[32,16,1024]{2,1,0:T(8,128)(2,1)}), bf16[32,16,1024]{2,1,0:T(8,128)(2,1)S(1)}, u32[]{:S(2)}, u32[]{:S(2)}) %all-to-all-start.3) | async-done | bytes 1048608 | tf_op jit(solution)/shard_map/all_to_all | solution.py:70
  381.0 0.8 convert_reduce_fusion
  381.8 59.0 %reduce-scatter.5.cloned.1.call-done = bf16[128,1024]{1,0:T(8,128)(2,1)} async-done(((bf16[4096,1024]{1,0:T(8,128)(2,1)}), bf16[128,1024]{1,0:T(8,128)(2,1)}) %reduce-scatter.5.cloned.1.call-update) | async-done | bytes 262160 | tf_op jit(solution)/shard_map/reduce_scatter | solution.py:139
  440.7 1.0 convert_bitcast_fusion
  441.7 1.0 copy.22
  (186 shorter events, 11.6 us)
Async XLA Ops:
  7.2 58.3 %copy-start = (bf16[384,512]{1,0:T(8,128)(2,1)S(1)}, bf16[384,512]{1,0:T(8,128)(2,1)}, u32[]{:S(2)}) copy-start(bf16[384,512]{1,0:T(8,128)(2,1)} %param.8) | copy-start | bytes 1179652
  7.2 58.3 %all-gather.4.cloned.1.call-start = ((), (), s32[]{:S(2)}) async-start(), calls=%async_computation.7 | async-start | bytes 1081344 | tf_op jit(solution)/shard_map/all_gather | solution.py:95
  7.9 141.8 %all-gather.6.cloned.1.call-start = ((), (), s32[]{:S(2)}) async-start(), calls=%async_computation.8 | async-start | bytes 8650752 | tf_op jit(solution)/shard_map/all_gather | solution.py:101
  8.7 195.6 %reduce-scatter.3.cloned.1.call-start = ((), (), s32[]{:S(2)}) async-start(), calls=%async_computation.9 | async-start | bytes 3538944 | tf_op jit(solution)/shard_map/reduce_scatter | solution.py:104
  157.9 0.7 copy-start.5
  157.9 3.2 copy-start.6
  157.9 3.2 copy-start.7
  157.9 47.6 %copy-start.4 = (bf16[512,8]{0,1:T(8,128)(2,1)S(1)}, bf16[512,8]{0,1:T(8,128)(2,1)}, u32[]{:S(2)}) copy-start(bf16[512,8]{0,1:T(8,128)(2,1)} %param.11) | copy-start | bytes 24580
  158.5 61.4 %copy-start.3 = (f32[8,384]{1,0:T(8,128)S(1)}, f32[8,384]{1,0:T(8,128)}, u32[]{:S(2)}) copy-start(f32[8,384]{1,0:T(8,128)} %param.12) | copy-start | bytes 36868
  159.7 52.1 %collective-permute-start = (s32[1]{0:T(128)}, s32[1]{0:T(128)}, u32[]{:S(2)}, u32[]{:S(2)}) collective-permute-start(s32[1]{0:T(128)} %add.218), channel_id=1, source_target_pairs={{8,0},{16,8},{24,16},{32,24},{40,32},{48,40},{56,48},{64,56},{72,6... | collective-permute-start | bytes 20 | tf_op jit(solution)/shard_map/ppermute | solution.py:21
  205.7 48.1 %copy-start.1 = (bf16[384,512]{1,0:T(8,128)(2,1)S(1)}, bf16[384,512]{1,0:T(8,128)(2,1)}, u32[]{:S(2)}) copy-start(bf16[384,512]{1,0:T(8,128)(2,1)} %reduce-scatter.3.cloned.1.call-done) | copy-start | bytes 1179652
  206.4 10.4 %all-to-all-start = ((f32[8,384,8]{1,2,0:T(8,128)}), f32[8,384,8]{1,2,0:T(8,128)S(1)}, u32[]{:S(2)}, u32[]{:S(2)}) async-start(f32[8,384,8]{1,2,0:T(8,128)} %broadcast_in_dim.26), calls=%async_computation.1 | async-start | bytes 196608 | tf_op jit(solution)/shard_map/all_to_all | solution.py:9
  216.9 3.1 collective-permute-start.1
  233.3 19.4 %all-to-all-start.1 = ((f32[32,2,8]{2,1,0:T(2,128)}), f32[32,2,8]{2,1,0:T(2,128)S(1)}, u32[]{:S(2)}, u32[]{:S(2)}) async-start(f32[32,2,8]{2,1,0:T(2,128)} %broadcast_in_dim.28), calls=%async_computation.2 | async-start | bytes 65536 | tf_op jit(solution)/shard_map/all_to_all | solution.py:9
  242.9 51.5 %all-gather.8.cloned.1.call-start = ((), (), s32[]{:S(2)}) async-start(), calls=%async_computation.10 | async-start | bytes 3538944 | tf_op jit(solution)/shard_map/all_gather | solution.py:127
  253.9 59.8 %copy-start.2 = (f32[8,384]{1,0:T(8,128)}, f32[8,384]{1,0:T(8,128)S(1)}, u32[]{:S(2)}) copy-start(f32[8,384]{1,0:T(8,128)S(1)} %get-tuple-element.26) | copy-start | bytes 36868
  255.1 185.7 %reduce-scatter.5.cloned.1.call-start = ((), (), s32[]{:S(2)}) async-start(), calls=%async_computation.11 | async-start | bytes 8650752 | tf_op jit(solution)/shard_map/reduce_scatter | solution.py:139
  304.5 18.8 %all-to-all-start.2 = ((f32[32,1,1]{2,1,0:T(1,128)}), f32[32,1,1]{2,1,0:T(1,128)S(1)}, u32[]{:S(2)}, u32[]{:S(2)}) async-start(f32[32,1,1]{2,1,0:T(1,128)} %broadcast_in_dim.52), calls=%async_computation.3 | async-start | bytes 32768 | tf_op jit(solution)/shard_map/all_to_all | solution.py:9
  324.2 22.0 %all-to-all-start.4 = ((f32[32,512,8]{1,2,0:T(8,128)}), f32[32,512,8]{1,2,0:T(8,128)S(1)}, u32[]{:S(2)}, u32[]{:S(2)}) async-start(f32[32,512,8]{1,2,0:T(8,128)} %broadcast_in_dim.53), calls=%async_computation.6 | async-start | bytes 1048576 | tf_op jit(solution)/shard_map/all_to_all | solution.py:9
  346.1 34.9 %all-to-all-start.3 = ((bf16[32,16,1024]{2,1,0:T(8,128)(2,1)}), bf16[32,16,1024]{2,1,0:T(8,128)(2,1)S(1)}, u32[]{:S(2)}, u32[]{:S(2)}) async-start(bf16[32,16,1024]{2,1,0:T(8,128)(2,1)} %bitcast.42), calls=%async_computation.4 | async-start | bytes 2097152 | tf_op jit(solution)/shard_map/all_to_all | solution.py:70
Sparse Core Ops, SparseCore 0:
  10.5 54.8 all-gather.3
  67.9 81.7 all-gather.5
  158.0 46.1 reduce-scatter.2
  255.2 39.1 all-gather.7
  303.3 137.3 reduce-scatter.4
where the time goes:
time: 451 us; the launch traced here: 450 us
  waiting for transfers between devices  343 us (76%)
  starting transfers between devices  35.1 us (8%)
  matrix products  30.4 us (7%)
  between operations  16.8 us (4%)
  local copies, waits for them, and re-layouts  16.5 us (4%)
  other arithmetic  8.07 us (2%)
    all_gather x1, waiting for transfers between devices, shards(): lax.all_gather(w_second, 'batch', axis=1, tiled=True)  82.4 us
    reduce_scatter x1, waiting for transfers between devices, shards(): lax.psum_scatter(contract(columns, hidden_first, 0, 0).astype(jnp.bfloat1...  59 us
    all_gather x1, waiting for transfers between devices, shards(): lax.all_gather(w_first, 'batch', axis=0, tiled=True)  56.7 us
    reduce_scatter x1, waiting for transfers between devices, shards(): lax.psum_scatter(partial_value.astype(jnp.bfloat16), 'hidden', scatter_di...  43.1 us
    all_gather x1, waiting for transfers between devices, shards(): slope_second = lax.all_gather(slope_share, 'hidden', axis=1, tiled=True)  39.2 us
    all_to_all x4, waiting for transfers between devices, sent_to_all(): lax.all_to_all(jnp.broadcast_to(array[None], (length, *array.shape)), axi...  31.2 us
    all_to_all x1, waiting for transfers between devices, summed_on_arrival(): lax.all_to_all(cut_along(array, dim, length), axis, 0, 0, tiled=True)  28.6 us
    all_to_all x4, starting transfers between devices, sent_to_all(): lax.all_to_all(jnp.broadcast_to(array[None], (length, *array.shape)), axi...  28 us
  transfers between devices with their start and end apart: 12, of which 11 were waited for; matrix products, arithmetic and copies ran while one was open for 4% of the time, Pallas kernels for 0%

commit v1 on v0

--- a/solution.py
+++ b/solution.py
@@ -124,7 +124,8 @@
     slope_share = (contract(slope_value, w_head, 1, 1) * silu_slope(pre_second)).astype(
         jnp.bfloat16
     )
-    slope_second = lax.all_gather(slope_share, "hidden", axis=1, tiled=True)
+    sent = jnp.stack([slope_share] * lax.axis_size("hidden"))
+    slope_second = jnp.concatenate(lax.all_to_all(sent, "hidden", 0, 0), axis=1)
     head_term = contract(hidden_second, slope_value, 0, 0)
     grad_head, loss_sum = (
         over_copies(head_term, "batch"),

time: 451 us -> 446 us (0.989)
  blocking collectives: 0 us -> 40.8 us
  waiting for transfers between devices: 343 us -> 304 us
  starting transfers between devices: 35.1 us -> 29.4 us
    all_to_all x0 -> x1, blocking collectives: none -> 40.8 us  [shards(): slope_second = jnp.concatenate(lax.all_to_all(sent, 'hidden', 0, 0), axis=1)]
    all_gather x1 -> x0, waiting for transfers between devices: 39.2 us -> none  [shards(): slope_second = lax.all_gather(slope_share, 'hidden', axis=1, tiled=True)]
    all_to_all x4, starting transfers between devices: 28 us -> 22.7 us  [sent_to_all(): lax.all_to_all(jnp.broadcast_to(array[None], (length, *array.shape)), axi...]
  transfers between devices with their start and end apart: 12 -> 11, of which waited for: 11 -> 10; matrix products, arithmetic and copies ran while one was open for 4% -> 5% of each run, Pallas kernels for 0% -> 0%
where the time goes in v1:
time: 446 us; the launch traced here: 445 us
  waiting for transfers between devices  304 us (68%)
  blocking collectives  40.8 us (9%)
  starting transfers between devices  29.4 us (7%)
  matrix products  27.8 us (6%)
  local copies, waits for them, and re-layouts  18.6 us (4%)
  between operations  16.8 us (4%)
  other arithmetic  8.08 us (2%)
    all_gather x1, waiting for transfers between devices, shards(): lax.all_gather(w_second, 'batch', axis=1, tiled=True)  82.4 us
    reduce_scatter x1, waiting for transfers between devices, shards(): lax.psum_scatter(contract(columns, hidden_first, 0, 0).astype(jnp.bfloat1...  57.8 us
    all_gather x1, waiting for transfers between devices, shards(): lax.all_gather(w_first, 'batch', axis=0, tiled=True)  56.7 us
    reduce_scatter x1, waiting for transfers between devices, shards(): lax.psum_scatter(partial_value.astype(jnp.bfloat16), 'hidden', scatter_di...  43.1 us
    all_to_all x1, blocking collectives, shards(): slope_second = jnp.concatenate(lax.all_to_all(sent, 'hidden', 0, 0), axis=1)  40.8 us
    all_to_all x4, waiting for transfers between devices, sent_to_all(): lax.all_to_all(jnp.broadcast_to(array[None], (length, *array.shape)), axi...  31.4 us
    all_to_all x1, waiting for transfers between devices, summed_on_arrival(): lax.all_to_all(cut_along(array, dim, length), axis, 0, 0, tiled=True)  29.1 us
    all_to_all x4, starting transfers between devices, sent_to_all(): lax.all_to_all(jnp.broadcast_to(array[None], (length, *array.shape)), axi...  22.7 us
  transfers between devices with their start and end apart: 11, of which 10 were waited for; matrix products, arithmetic and copies ran while one was open for 5% of the time, Pallas kernels for 0%

profile of v1, /device:TPU:8, one launch (start us, length us, event | category | flops | bytes accessed | tf_op | source)
XLA Modules:
  0.0 445.4 jit_solution(14820151505460503589)
XLA Ops:
  7.2 0.7 all-gather.3.cloned.1.call-update
  8.0 0.7 all-gather.5.cloned.1.call-update
  8.7 56.7 %all-gather.3.cloned.1.call-done = bf16[512,1024]{1,0:T(8,128)(2,1)} async-done(((bf16[16,1024]{1,0:T(8,128)(2,1)}), bf16[512,1024]{1,0:T(8,128)(2,1)}) %all-gather.3.cloned.1.call-update) | async-done | bytes 1048592 | tf_op jit(solution)/shard_map/all_gather | solution.py:95
  65.5 1.8 fusion.20
  67.3 82.4 %all-gather.5.cloned.1.call-done = bf16[1024,4096]{1,0:T(8,128)(2,1)} async-done(((bf16[1024,128]{1,0:T(8,128)(2,1)}), bf16[1024,4096]{1,0:T(8,128)(2,1)}) %all-gather.5.cloned.1.call-update) | async-done | bytes 8388624 | tf_op jit(solution)/shard_map/all_gather | solution.py:101
  149.7 8.2 %convolution_convert_fusion.1 = bf16[384,4096]{1,0:T(8,128)(2,1)} fusion(bf16[1024,4096]{1,0:T(8,128)(2,1)} %all-gather.5.cloned.1.call-done, f32[384,1024]{1,0:T(8,128)S(1)} %fusion.20), kind=kOutput, calls=%fused_computation.1 | convolution fusion | flops 3224764416 | bytes 13107200 | tf_op jit(solution)/shard_map/dot_general | solution.py:99
  157.9 0.6 copy-done.6
  158.5 0.5 slice.355
  159.7 1.3 collective-permute-start
  161.1 43.1 %reduce-scatter.3.cloned.1.call-done = bf16[384,512]{1,0:T(8,128)(2,1)} async-done(((bf16[384,4096]{1,0:T(8,128)(2,1)}), bf16[384,512]{1,0:T(8,128)(2,1)}) %reduce-scatter.3.cloned.1.call-update) | async-done | bytes 393232 | tf_op jit(solution)/shard_map/reduce_scatter | solution.py:104
  204.3 1.2 fusion.4
  205.7 0.7 broadcast_in_dim.26
  206.4 5.4 %all-to-all-start = ((f32[8,384,8]{1,2,0:T(8,128)}), f32[8,384,8]{1,2,0:T(8,128)S(1)}, u32[]{:S(2)}, u32[]{:S(2)}) async-start(f32[8,384,8]{1,2,0:T(8,128)} %broadcast_in_dim.26), calls=%async_computation.1 | async-start | bytes 196608 | tf_op jit(solution)/shard_map/all_to_all | solution.py:9
  211.8 0.6 fusion.12
  212.4 4.3 all-to-all-done
  216.9 1.3 collective-permute-start.1
  218.2 1.8 collective-permute-done.1
  220.1 0.3 slice.371
  220.4 0.3 slice.365
  220.6 0.3 slice.361
  221.9 0.3 slice.367
  222.2 0.3 slice.363
  222.4 0.3 slice.359
  231.3 0.3 pad.128
  232.6 0.6 broadcast_in_dim.28
  233.3 9.6 %all-to-all-start.1 = ((f32[32,2,8]{2,1,0:T(2,128)}), f32[32,2,8]{2,1,0:T(2,128)S(1)}, u32[]{:S(2)}, u32[]{:S(2)}) async-start(f32[32,2,8]{2,1,0:T(2,128)} %broadcast_in_dim.28), calls=%async_computation.2 | async-start | bytes 65536 | tf_op jit(solution)/shard_map/all_to_all | solution.py:9
  243.4 9.3 %all-to-all-done.1 = f32[32,2,8]{2,1,0:T(2,128)S(1)} async-done(((f32[32,2,8]{2,1,0:T(2,128)}), f32[32,2,8]{2,1,0:T(2,128)S(1)}, u32[]{:S(2)}, u32[]{:S(2)}) %all-to-all-start.1) | async-done | bytes 2080 | tf_op jit(solution)/shard_map/all_to_all | solution.py:9
  253.2 0.7 multiply_reduce_fusion
  253.9 0.4 fusion
  254.5 0.3 stack.2
  254.8 40.8 %all_to_all.31 = bf16[8,384,512]{1,2,0:T(8,128)(2,1)S(1)} all-to-all(bf16[8,384,512]{1,2,0:T(8,128)(2,1)S(1)} %stack.2), channel_id=1, replica_groups=mesh['batch'=32,'hidden'=8] {'hidden'}, dimensions={0} | all-to-all | bytes 6291456 | tf_op jit(solution)/shard_map/all_to_all | solution.py:128
  295.6 1.6 copy-done.1
  297.2 6.9 %convolution_convert_fusion = bf16[4096,1024]{1,0:T(8,128)(2,1)} fusion(bf16[384,4096]{0,1:T(8,128)(2,1)S(1)} %bitcast.45, f32[384,1024]{1,0:T(8,128)S(1)} %fusion.20), kind=kOutput, calls=%fused_computation | convolution fusion | flops 3227385856 | bytes 13107200 | tf_op jit(solution)/shard_map/dot_general | solution.py:84
  304.2 1.3 broadcast_in_dim.52
  305.4 3.8 all-to-all-start.2
  309.4 9.6 %all-to-all-done.2 = f32[32,1,1]{2,1,0:T(1,128)S(1)} async-done(((f32[32,1,1]{2,1,0:T(1,128)}), f32[32,1,1]{2,1,0:T(1,128)S(1)}, u32[]{:S(2)}, u32[]{:S(2)}) %all-to-all-start.2) | async-done | bytes 160 | tf_op jit(solution)/shard_map/all_to_all | solution.py:9
  319.0 0.9 broadcast_in_dim.53
  319.8 3.9 all-to-all-start.5
  323.7 10.1 %convolution_convert_fusion.2 = bf16[1024,512]{0,1:T(8,128)(2,1)} fusion(bf16[384,512]{1,0:T(8,128)(2,1)S(1)} %copy-done, f32[384,1024]{1,0:T(8,128)S(1)} %fusion.20, bf16[384,4096]{0,1:T(8,128)(2,1)} %bitcast.46, bf16[1024,4096]{1,0:T(8,128)(2,1)} %all-gather.5.cloned.1.call-done), kind=kOutput, calls=%fused_computation.6 | convolution fusion | flops 3627941888 | bytes 14548992 | tf_op jit(solution)/shard_map/dot_general | solution.py:84
  333.8 8.2 %all-to-all-done.5 = f32[32,512,8]{1,2,0:T(8,128)S(1)} async-done(((f32[32,512,8]{1,2,0:T(8,128)}), f32[32,512,8]{1,2,0:T(8,128)S(1)}, u32[]{:S(2)}, u32[]{:S(2)}) %all-to-all-start.5) | async-done | bytes 524320 | tf_op jit(solution)/shard_map/all_to_all | solution.py:9
  342.0 4.0 all-to-all-start.4
  346.0 0.6 reduce_sum.47
  347.3 0.7 reduce_sum.49
  348.0 29.1 %all-to-all-done.4 = bf16[32,16,1024]{2,1,0:T(8,128)(2,1)S(1)} async-done(((bf16[32,16,1024]{2,1,0:T(8,128)(2,1)}), bf16[32,16,1024]{2,1,0:T(8,128)(2,1)S(1)}, u32[]{:S(2)}, u32[]{:S(2)}) %all-to-all-start.4) | async-done | bytes 1048608 | tf_op jit(solution)/shard_map/all_to_all | solution.py:70
  377.1 0.8 convert_reduce_fusion
  377.9 57.8 %reduce-scatter.5.cloned.1.call-done = bf16[128,1024]{1,0:T(8,128)(2,1)} async-done(((bf16[4096,1024]{1,0:T(8,128)(2,1)}), bf16[128,1024]{1,0:T(8,128)(2,1)}) %reduce-scatter.5.cloned.1.call-update) | async-done | bytes 262160 | tf_op jit(solution)/shard_map/reduce_scatter | solution.py:140
  435.7 1.0 convert_bitcast_fusion
  436.7 1.0 copy.29
  (188 shorter events, 12.3 us)
Async XLA Ops:
  7.2 58.3 %copy-start = (bf16[384,512]{1,0:T(8,128)(2,1)S(1)}, bf16[384,512]{1,0:T(8,128)(2,1)}, u32[]{:S(2)}) copy-start(bf16[384,512]{1,0:T(8,128)(2,1)} %param.8) | copy-start | bytes 1179652
  7.2 58.3 %all-gather.3.cloned.1.call-start = ((), (), s32[]{:S(2)}) async-start(), calls=%async_computation.8 | async-start | bytes 1081344 | tf_op jit(solution)/shard_map/all_gather | solution.py:95
  7.9 141.8 %all-gather.5.cloned.1.call-start = ((), (), s32[]{:S(2)}) async-start(), calls=%async_computation.9 | async-start | bytes 8650752 | tf_op jit(solution)/shard_map/all_gather | solution.py:101
  8.7 195.6 %reduce-scatter.3.cloned.1.call-start = ((), (), s32[]{:S(2)}) async-start(), calls=%async_computation.10 | async-start | bytes 3538944 | tf_op jit(solution)/shard_map/reduce_scatter | solution.py:104
  157.9 0.7 copy-start.6
  157.9 3.2 copy-start.7
  157.9 3.2 copy-start.8
  157.9 47.6 %copy-start.5 = (bf16[512,8]{0,1:T(8,128)(2,1)S(1)}, bf16[512,8]{0,1:T(8,128)(2,1)}, u32[]{:S(2)}) copy-start(bf16[512,8]{0,1:T(8,128)(2,1)} %param.11) | copy-start | bytes 24580
  158.5 61.4 %copy-start.4 = (f32[8,384]{1,0:T(8,128)S(1)}, f32[8,384]{1,0:T(8,128)}, u32[]{:S(2)}) copy-start(f32[8,384]{1,0:T(8,128)} %param.12) | copy-start | bytes 36868
  159.7 52.1 %collective-permute-start = (s32[1]{0:T(128)}, s32[1]{0:T(128)}, u32[]{:S(2)}, u32[]{:S(2)}) collective-permute-start(s32[1]{0:T(128)} %add.218), channel_id=1, source_target_pairs={{8,0},{16,8},{24,16},{32,24},{40,32},{48,40},{56,48},{64,56},{72,6... | collective-permute-start | bytes 20 | tf_op jit(solution)/shard_map/ppermute | solution.py:21
  205.7 48.1 %copy-start.2 = (bf16[384,512]{1,0:T(8,128)(2,1)S(1)}, bf16[384,512]{1,0:T(8,128)(2,1)}, u32[]{:S(2)}) copy-start(bf16[384,512]{1,0:T(8,128)(2,1)} %reduce-scatter.3.cloned.1.call-done) | copy-start | bytes 1179652
  206.4 10.4 %all-to-all-start = ((f32[8,384,8]{1,2,0:T(8,128)}), f32[8,384,8]{1,2,0:T(8,128)S(1)}, u32[]{:S(2)}, u32[]{:S(2)}) async-start(f32[8,384,8]{1,2,0:T(8,128)} %broadcast_in_dim.26), calls=%async_computation.1 | async-start | bytes 196608 | tf_op jit(solution)/shard_map/all_to_all | solution.py:9
  216.9 3.1 collective-permute-start.1
  233.3 19.4 %all-to-all-start.1 = ((f32[32,2,8]{2,1,0:T(2,128)}), f32[32,2,8]{2,1,0:T(2,128)S(1)}, u32[]{:S(2)}, u32[]{:S(2)}) async-start(f32[32,2,8]{2,1,0:T(2,128)} %broadcast_in_dim.28), calls=%async_computation.2 | async-start | bytes 65536 | tf_op jit(solution)/shard_map/all_to_all | solution.py:9
  242.8 192.9 %reduce-scatter.5.cloned.1.call-start = ((), (), s32[]{:S(2)}) async-start(), calls=%async_computation.11 | async-start | bytes 8650752 | tf_op jit(solution)/shard_map/reduce_scatter | solution.py:140
  253.8 55.4 %copy-start.3 = (f32[8,384]{1,0:T(8,128)}, f32[8,384]{1,0:T(8,128)S(1)}, u32[]{:S(2)}) copy-start(f32[8,384]{1,0:T(8,128)S(1)} %get-tuple-element.31) | copy-start | bytes 36868
  295.6 1.6 copy-start.1
  305.4 13.6 %all-to-all-start.2 = ((f32[32,1,1]{2,1,0:T(1,128)}), f32[32,1,1]{2,1,0:T(1,128)S(1)}, u32[]{:S(2)}, u32[]{:S(2)}) async-start(f32[32,1,1]{2,1,0:T(1,128)} %broadcast_in_dim.52), calls=%async_computation.3 | async-start | bytes 32768 | tf_op jit(solution)/shard_map/all_to_all | solution.py:9
  319.8 22.2 %all-to-all-start.5 = ((f32[32,512,8]{1,2,0:T(8,128)}), f32[32,512,8]{1,2,0:T(8,128)S(1)}, u32[]{:S(2)}, u32[]{:S(2)}) async-start(f32[32,512,8]{1,2,0:T(8,128)} %broadcast_in_dim.53), calls=%async_computation.7 | async-start | bytes 1048576 | tf_op jit(solution)/shard_map/all_to_all | solution.py:9
  342.0 35.1 %all-to-all-start.4 = ((bf16[32,16,1024]{2,1,0:T(8,128)(2,1)}), bf16[32,16,1024]{2,1,0:T(8,128)(2,1)S(1)}, u32[]{:S(2)}, u32[]{:S(2)}) async-start(bf16[32,16,1024]{2,1,0:T(8,128)(2,1)} %bitcast.47), calls=%async_computation.5 | async-start | bytes 2097152 | tf_op jit(solution)/shard_map/all_to_all | solution.py:70
Sparse Core Ops, SparseCore 0:
  10.5 54.8 all-gather.2
  67.9 81.7 all-gather.4
  158.0 46.1 reduce-scatter.2
  304.3 131.4 reduce-scatter.4
